TPU v7x, 256 devices: a whole 4x4x8 slice. The times are simulated.
256 devices in a mesh: ctx: 32 (over z, x_hi, core), head: 8 (over y, x_lo).
Axes of the slice: x: 4 (x_hi: 2, x_lo: 2; x = x_hi * 2 + x_lo), y: 4, z: 8, core: 2. Of those that a mesh axis runs over, the one named last changes fastest.
Arguments:
- query_heads: bfloat16 [8192, 32, 128], P('ctx', 'head'), may hold values from -5 to 5
- key_heads: bfloat16 [8192, 16, 128], P('ctx', 'head'), may hold values from -5 to 5
- value_heads: bfloat16 [8192, 16, 128], P('ctx', 'head'), may hold values from -6 to 6
- positions: int32 [8192], P('ctx'), may hold values from 0 to 8191, each once
- out_weight: bfloat16 [4096, 4608], P('head'), may hold values from -0.125 to 0.125
Outputs:
- attn_out: bfloat16 [8192, 4608], P('ctx', 'head')
Inputs may be any that keep to these rules, and one draw needn't show every extreme that they name: Each of the 8192 positions appears exactly once.
All inputs are finite; a program needn't handle non-finite values.
Results may differ from a plain program's by a relative error of at most 0.0081.
Values may be sent and summed in bfloat16 or wider, within the bound.
A program may use at most 64 MiB of HBM per device.

v0:
```python
import math

import jax
import jax.numpy as jnp
from jax import lax
from jax.sharding import Mesh
from jax.sharding import PartitionSpec as P

CTX = ("ctx_0", "ctx_1", "ctx_2")


NEG_BIG = -1e30
ATTN_SCALE = 1.0 / 12.0


def joined_along(pieces, dim):
    dims = list(pieces.shape[1:])
    dims[dim] *= pieces.shape[0]
    return jnp.moveaxis(pieces, 0, dim).reshape(dims)


def stacked_from(shard, axes, turns):
    pieces = shard
    for k in turns:
        pieces = lax.all_gather(pieces, axes[k])
    done = turns[::-1]
    back = [done.index(k) for k in range(len(axes))]
    pieces = pieces.transpose(*back, *range(len(axes), pieces.ndim))
    return pieces.reshape(-1, *shard.shape)


def gather_axes(shard, axes, turns, dim):
    return joined_along(stacked_from(shard, axes, turns), dim)


def in_one_piece(arrays, axis, dim, along):
    both = jnp.concatenate(arrays, axis=along)
    out, at, gathered = (lax.all_gather(both, axis, axis=dim, tiled=True), 0, [])
    for a in arrays:
        gathered.append(lax.slice_in_dim(out, at, at + a.shape[along], axis=along))
        at += a.shape[along]
    return tuple(gathered)


def in_blocks(shard, dim, count):
    before, after = (shard.shape[:dim], shard.shape[dim + 1 :])
    return jnp.moveaxis(shard.reshape(*before, count, -1, *after), dim, 0)


def sent_and_summed(shard, axis, dim):
    pieces = in_blocks(shard, dim, lax.axis_size(axis))
    arrived = lax.all_to_all(pieces, axis, split_axis=0, concat_axis=0, tiled=True)
    return arrived.astype(jnp.float32).sum(axis=0)


def on_device(query_heads, key_heads, value_heads, positions, out_weight):
    tok_local, heads_local, head_size = query_heads.shape
    kv_local = key_heads.shape[1]
    group_size = heads_local // kv_local
    grouped = query_heads.reshape(tok_local, kv_local, group_size, head_size)
    all_positions = gather_axes(positions, (("ctx_0", "ctx_1"), "ctx_2"), (0, 1), 0)
    stat_shape = (kv_local, group_size, tok_local)
    initial = (
        jnp.full(stat_shape, NEG_BIG, jnp.float32),
        jnp.zeros(stat_shape, jnp.float32),
        jnp.zeros(stat_shape + (head_size,), jnp.float32),
    )

    def attend_block(carry, key_block, value_block, key_pos):
        running_max, running_sum, accum = carry
        scores = (
            jnp.einsum("tkgd,skd->kgts", grouped, key_block, preferred_element_type=jnp.float32)
            * ATTN_SCALE
        )
        visible = key_pos[None, :] <= positions[:, None]
        scores = jnp.where(visible, scores, NEG_BIG)
        new_max = jnp.maximum(running_max, jnp.max(scores, axis=-1))
        weights = jnp.where(visible, jnp.exp(scores - new_max[..., None]), 0.0)
        decay_old = jnp.exp(running_max - new_max)
        running_sum = running_sum * decay_old + jnp.sum(weights, axis=-1)
        accum = accum * decay_old[..., None] + jnp.einsum(
            "kgts,skd->kgtd",
            weights.astype(jnp.bfloat16),
            value_block,
            preferred_element_type=jnp.float32,
        )
        return (new_max, running_sum, accum)

    key_piece, value_piece = in_one_piece((key_heads, value_heads), CTX, 0, 1)
    piece_rows = key_piece.shape[0]
    block_rows = math.gcd(piece_rows, 1024)

    def one_block(inner, block_index):
        offset = block_index * block_rows
        key_block = lax.dynamic_slice_in_dim(key_piece, offset, block_rows, 0)
        value_block = lax.dynamic_slice_in_dim(value_piece, offset, block_rows, 0)
        key_pos = lax.dynamic_slice_in_dim(all_positions, offset, block_rows, 0)
        return (attend_block(inner, key_block, value_block, key_pos), None)

    result, _ = lax.scan(one_block, initial, jnp.arange(piece_rows // block_rows, dtype=jnp.int32))
    _, total, accum = result
    attended = (accum / total[..., None]).astype(jnp.bfloat16)
    flat = jnp.transpose(attended, (2, 0, 1, 3)).reshape(tok_local, heads_local * head_size)
    terms = jnp.dot(flat, out_weight, preferred_element_type=jnp.float32)
    return sent_and_summed(terms.astype(jnp.bfloat16), "head", 1).astype(jnp.bfloat16)


def solution(mesh):
    torus = Mesh(
        mesh.devices.reshape(8, 2, 2, mesh.shape["head"]), ("ctx_0", "ctx_1", "ctx_2", "head")
    )
    return jax.shard_map(
        on_device,
        mesh=torus,
        in_specs=(
            P(CTX, "head", None),
            P(CTX, "head", None),
            P(CTX, "head", None),
            P(CTX),
            P("head", None),
        ),
        out_specs=P(CTX, "head"),
        check_vma=False,
    )
```

profile of v0, /device:TPU:1, one launch (start us, length us, event | category | flops | bytes accessed | tf_op | source)
XLA Modules:
  0.0 259.9 jit_solution(15289566431084043918)
XLA Ops:
  6.5 0.9 copy.25
  7.5 0.9 copy.26
  8.4 0.7 pad_maximum_fusion
  9.1 0.0 all-gather.5.cloned.1.call-update
  9.2 1.0 copy.27
  10.2 37.7 %all-gather.2 = s32[16,1,256]{2,1,0:T(1,128)S(1)} all-gather(s32[1,1,256]{2,1,0:T(1,128)} %bitcast.68), channel_id=2, replica_groups=mesh['ctx_0'=8,'ctx_1'=2,'ctx_2'=2,'head'=8] {'ctx_0','ctx_1'}, dimensions={0}, use_global_device_ids=true | all-gather | bytes 17408 | tf_op jit(solution)/shard_map/all_gather | solution.py:25
  47.9 9.4 %all-gather.1 = s32[32,256]{1,0:T(8,128)S(1)} all-gather(s32[16,256]{1,0:T(8,128)S(1)} %bitcast.67), channel_id=3, replica_groups=mesh['ctx_0'=8,'ctx_1'=2,'ctx_2'=2,'head'=8] {'ctx_2'}, dimensions={0}, use_global_device_ids=true | all-gather | bytes 49152 | tf_op jit(solution)/shard_map/all_gather | solution.py:25
  57.3 0.0 copy-start.1
  57.4 58.1 %all-gather.5.cloned.1.call-done = bf16[8192,4,128]{2,0,1:T(8,128)(2,1)} async-done(((bf16[256,4,128]{2,0,1:T(8,128)(2,1)}), bf16[8192,4,128]{2,0,1:T(8,128)(2,1)}) %all-gather.5.cloned.1.call-update) | async-done | bytes 8388624 | tf_op jit(solution)/shard_map/all_gather | solution.py:38
  115.4 5.7 %fusion.21 = (bf16[8192,2,128]{2,0,1:T(8,128)(2,1)}, bf16[8192,2,128]{2,0,1:T(8,128)(2,1)}) fusion(bf16[8192,4,128]{2,0,1:T(8,128)(2,1)} %all-gather.5.cloned.1.call-done), kind=kLoop, calls=%fused_computation.30 | loop fusion | bytes 16777216 | tf_op jit(solution)/shard_map/slice | solution.py:40
  121.1 91.4 %while.15 = (s32[]{:T(128)}, f32[2,2,256]{2,1,0:T(2,128)S(1)}, f32[2,2,256]{2,1,0:T(2,128)S(1)}, f32[2,2,256,128]{3,2,1,0:T(8,128)S(1)}, s32[8]{0:T(128)S(1)}, /...) while((s32[]{:T(128)}, f32[2,2,256]{2,1,0:T(2,128)S(1)}, ...), condition=%wide.region_3.4_spmd.clone, body=%wide.region_0.3_spmd.clone.sunk | while | flops 551162880 | bytes 32847088 | solution.py:100
  121.1 0.6 dynamic_slice.33
  122.4 0.2 broadcast_compare_fusion.2
  122.6 3.8 %fusion.36 = (f32[2,2,256]{2,1,0:T(2,128)S(1)}, f32[2,1024,256,2]{2,1,3,0:T(8,128)}) fusion(pred[256,1024]{0,1:T(8,128)(4,1)S(1)} %broadcast_compare_fusion.2, bf16[256,2,2,128]{3,0,2,1:T(8,128)(2,1)S(1)} %get-tuple-element.224, bf16[8192,2,128]{2,0,1:T(8,128)(2,1)} %get-tuple-element.223, s32[]{:T(128)S(6)} %select_n.46), kind=kOutput, calls=%fused_computation.2.clone.1 | convolution fusion | flops 271580160 | bytes 5246980 | tf_op jit(solution)/shard_map/while/body/eval_jaxpr/tkgd,skd->kgts/dot_general | solution.py:72
  126.4 3.4 %fusion.38 = f32[2,2,256]{2,1,0:T(2,128)S(1)} fusion(f32[2,1024,256,2]{2,1,3,0:T(8,128)} %get-tuple-element.185, f32[2,2,256]{2,1,0:T(2,128)S(1)} %fusion.37, pred[256,1024]{0,1:T(8,128)(4,1)S(1)} %broadcast_compare_fusion.2), kind=kLoop, calls=%fused_computation.4.clone.1 | loop fusion | flops 5241856 | bytes 4464640 | tf_op jit(solution)/shard_map/while/body/eval_jaxpr/reduce_sum | solution.py:80
  129.8 0.0 copy-done
  129.9 2.7 %fusion.40 = f32[2,2,256,128]{3,2,1,0:T(8,128)S(1)} fusion(f32[2,1024,256,2]{2,1,3,0:T(8,128)S(1)} %copy-done, f32[2,2,256]{2,1,0:T(2,128)S(1)} %fusion.37, pred[256,1024]{0,1:T(8,128)(4,1)S(1)} %broadcast_compare_fusion.2, f32[2,2,256,128]{3,2,1,0:T(8,128)S(1)} %get-tuple-element.205, bf16[8192,2,128]{2,0,1:T(8,128)(2,1)} %get-tuple-element.225, ...), kind=kOutput, calls=%fused_computation.7.clone.1 | convolution fusion | flops 274071552 | bytes 6037509 | tf_op jit(solution)/shard_map/while/body/eval_jaxpr/kgts,skd->kgtd/dot_general | solution.py:81
  132.6 0.6 dynamic_slice.33
  133.8 0.2 broadcast_compare_fusion.2
  134.0 3.8 %fusion.36 = (f32[2,2,256]{2,1,0:T(2,128)S(1)}, f32[2,1024,256,2]{2,1,3,0:T(8,128)}) fusion(pred[256,1024]{0,1:T(8,128)(4,1)S(1)} %broadcast_compare_fusion.2, bf16[256,2,2,128]{3,0,2,1:T(8,128)(2,1)S(1)} %get-tuple-element.224, bf16[8192,2,128]{2,0,1:T(8,128)(2,1)} %get-tuple-element.223, s32[]{:T(128)S(6)} %select_n.46), kind=kOutput, calls=%fused_computation.2.clone.1 | convolution fusion | flops 271580160 | bytes 5246980 | tf_op jit(solution)/shard_map/while/body/eval_jaxpr/tkgd,skd->kgts/dot_general | solution.py:72
  137.8 3.4 %fusion.38 = f32[2,2,256]{2,1,0:T(2,128)S(1)} fusion(f32[2,1024,256,2]{2,1,3,0:T(8,128)} %get-tuple-element.185, f32[2,2,256]{2,1,0:T(2,128)S(1)} %fusion.37, pred[256,1024]{0,1:T(8,128)(4,1)S(1)} %broadcast_compare_fusion.2), kind=kLoop, calls=%fused_computation.4.clone.1 | loop fusion | flops 5241856 | bytes 4464640 | tf_op jit(solution)/shard_map/while/body/eval_jaxpr/reduce_sum | solution.py:80
  141.2 0.0 copy-done
  141.3 2.7 %fusion.40 = f32[2,2,256,128]{3,2,1,0:T(8,128)S(1)} fusion(f32[2,1024,256,2]{2,1,3,0:T(8,128)S(1)} %copy-done, f32[2,2,256]{2,1,0:T(2,128)S(1)} %fusion.37, pred[256,1024]{0,1:T(8,128)(4,1)S(1)} %broadcast_compare_fusion.2, f32[2,2,256,128]{3,2,1,0:T(8,128)S(1)} %get-tuple-element.205, bf16[8192,2,128]{2,0,1:T(8,128)(2,1)} %get-tuple-element.225, ...), kind=kOutput, calls=%fused_computation.7.clone.1 | convolution fusion | flops 274071552 | bytes 6037509 | tf_op jit(solution)/shard_map/while/body/eval_jaxpr/kgts,skd->kgtd/dot_general | solution.py:81
  144.0 0.6 dynamic_slice.33
  145.2 0.2 broadcast_compare_fusion.2
  145.5 3.8 %fusion.36 = (f32[2,2,256]{2,1,0:T(2,128)S(1)}, f32[2,1024,256,2]{2,1,3,0:T(8,128)}) fusion(pred[256,1024]{0,1:T(8,128)(4,1)S(1)} %broadcast_compare_fusion.2, bf16[256,2,2,128]{3,0,2,1:T(8,128)(2,1)S(1)} %get-tuple-element.224, bf16[8192,2,128]{2,0,1:T(8,128)(2,1)} %get-tuple-element.223, s32[]{:T(128)S(6)} %select_n.46), kind=kOutput, calls=%fused_computation.2.clone.1 | convolution fusion | flops 271580160 | bytes 5246980 | tf_op jit(solution)/shard_map/while/body/eval_jaxpr/tkgd,skd->kgts/dot_general | solution.py:72
  149.3 3.4 %fusion.38 = f32[2,2,256]{2,1,0:T(2,128)S(1)} fusion(f32[2,1024,256,2]{2,1,3,0:T(8,128)} %get-tuple-element.185, f32[2,2,256]{2,1,0:T(2,128)S(1)} %fusion.37, pred[256,1024]{0,1:T(8,128)(4,1)S(1)} %broadcast_compare_fusion.2), kind=kLoop, calls=%fused_computation.4.clone.1 | loop fusion | flops 5241856 | bytes 4464640 | tf_op jit(solution)/shard_map/while/body/eval_jaxpr/reduce_sum | solution.py:80
  152.7 0.0 copy-done
  152.7 2.7 %fusion.40 = f32[2,2,256,128]{3,2,1,0:T(8,128)S(1)} fusion(f32[2,1024,256,2]{2,1,3,0:T(8,128)S(1)} %copy-done, f32[2,2,256]{2,1,0:T(2,128)S(1)} %fusion.37, pred[256,1024]{0,1:T(8,128)(4,1)S(1)} %broadcast_compare_fusion.2, f32[2,2,256,128]{3,2,1,0:T(8,128)S(1)} %get-tuple-element.205, bf16[8192,2,128]{2,0,1:T(8,128)(2,1)} %get-tuple-element.225, ...), kind=kOutput, calls=%fused_computation.7.clone.1 | convolution fusion | flops 274071552 | bytes 6037509 | tf_op jit(solution)/shard_map/while/body/eval_jaxpr/kgts,skd->kgtd/dot_general | solution.py:81
  155.4 0.6 dynamic_slice.33
  156.7 0.2 broadcast_compare_fusion.2
  156.9 3.8 %fusion.36 = (f32[2,2,256]{2,1,0:T(2,128)S(1)}, f32[2,1024,256,2]{2,1,3,0:T(8,128)}) fusion(pred[256,1024]{0,1:T(8,128)(4,1)S(1)} %broadcast_compare_fusion.2, bf16[256,2,2,128]{3,0,2,1:T(8,128)(2,1)S(1)} %get-tuple-element.224, bf16[8192,2,128]{2,0,1:T(8,128)(2,1)} %get-tuple-element.223, s32[]{:T(128)S(6)} %select_n.46), kind=kOutput, calls=%fused_computation.2.clone.1 | convolution fusion | flops 271580160 | bytes 5246980 | tf_op jit(solution)/shard_map/while/body/eval_jaxpr/tkgd,skd->kgts/dot_general | solution.py:72
  160.7 3.4 %fusion.38 = f32[2,2,256]{2,1,0:T(2,128)S(1)} fusion(f32[2,1024,256,2]{2,1,3,0:T(8,128)} %get-tuple-element.185, f32[2,2,256]{2,1,0:T(2,128)S(1)} %fusion.37, pred[256,1024]{0,1:T(8,128)(4,1)S(1)} %broadcast_compare_fusion.2), kind=kLoop, calls=%fused_computation.4.clone.1 | loop fusion | flops 5241856 | bytes 4464640 | tf_op jit(solution)/shard_map/while/body/eval_jaxpr/reduce_sum | solution.py:80
  164.1 0.0 copy-done
  164.1 2.7 %fusion.40 = f32[2,2,256,128]{3,2,1,0:T(8,128)S(1)} fusion(f32[2,1024,256,2]{2,1,3,0:T(8,128)S(1)} %copy-done, f32[2,2,256]{2,1,0:T(2,128)S(1)} %fusion.37, pred[256,1024]{0,1:T(8,128)(4,1)S(1)} %broadcast_compare_fusion.2, f32[2,2,256,128]{3,2,1,0:T(8,128)S(1)} %get-tuple-element.205, bf16[8192,2,128]{2,0,1:T(8,128)(2,1)} %get-tuple-element.225, ...), kind=kOutput, calls=%fused_computation.7.clone.1 | convolution fusion | flops 274071552 | bytes 6037509 | tf_op jit(solution)/shard_map/while/body/eval_jaxpr/kgts,skd->kgtd/dot_general | solution.py:81
  166.8 0.6 dynamic_slice.33
  168.1 0.2 broadcast_compare_fusion.2
  168.3 3.8 %fusion.36 = (f32[2,2,256]{2,1,0:T(2,128)S(1)}, f32[2,1024,256,2]{2,1,3,0:T(8,128)}) fusion(pred[256,1024]{0,1:T(8,128)(4,1)S(1)} %broadcast_compare_fusion.2, bf16[256,2,2,128]{3,0,2,1:T(8,128)(2,1)S(1)} %get-tuple-element.224, bf16[8192,2,128]{2,0,1:T(8,128)(2,1)} %get-tuple-element.223, s32[]{:T(128)S(6)} %select_n.46), kind=kOutput, calls=%fused_computation.2.clone.1 | convolution fusion | flops 271580160 | bytes 5246980 | tf_op jit(solution)/shard_map/while/body/eval_jaxpr/tkgd,skd->kgts/dot_general | solution.py:72
  172.1 3.4 %fusion.38 = f32[2,2,256]{2,1,0:T(2,128)S(1)} fusion(f32[2,1024,256,2]{2,1,3,0:T(8,128)} %get-tuple-element.185, f32[2,2,256]{2,1,0:T(2,128)S(1)} %fusion.37, pred[256,1024]{0,1:T(8,128)(4,1)S(1)} %broadcast_compare_fusion.2), kind=kLoop, calls=%fused_computation.4.clone.1 | loop fusion | flops 5241856 | bytes 4464640 | tf_op jit(solution)/shard_map/while/body/eval_jaxpr/reduce_sum | solution.py:80
  175.5 0.0 copy-done
  175.5 2.7 %fusion.40 = f32[2,2,256,128]{3,2,1,0:T(8,128)S(1)} fusion(f32[2,1024,256,2]{2,1,3,0:T(8,128)S(1)} %copy-done, f32[2,2,256]{2,1,0:T(2,128)S(1)} %fusion.37, pred[256,1024]{0,1:T(8,128)(4,1)S(1)} %broadcast_compare_fusion.2, f32[2,2,256,128]{3,2,1,0:T(8,128)S(1)} %get-tuple-element.205, bf16[8192,2,128]{2,0,1:T(8,128)(2,1)} %get-tuple-element.225, ...), kind=kOutput, calls=%fused_computation.7.clone.1 | convolution fusion | flops 274071552 | bytes 6037509 | tf_op jit(solution)/shard_map/while/body/eval_jaxpr/kgts,skd->kgtd/dot_general | solution.py:81
  178.2 0.6 dynamic_slice.33
  179.5 0.2 broadcast_compare_fusion.2
  179.7 3.8 %fusion.36 = (f32[2,2,256]{2,1,0:T(2,128)S(1)}, f32[2,1024,256,2]{2,1,3,0:T(8,128)}) fusion(pred[256,1024]{0,1:T(8,128)(4,1)S(1)} %broadcast_compare_fusion.2, bf16[256,2,2,128]{3,0,2,1:T(8,128)(2,1)S(1)} %get-tuple-element.224, bf16[8192,2,128]{2,0,1:T(8,128)(2,1)} %get-tuple-element.223, s32[]{:T(128)S(6)} %select_n.46), kind=kOutput, calls=%fused_computation.2.clone.1 | convolution fusion | flops 271580160 | bytes 5246980 | tf_op jit(solution)/shard_map/while/body/eval_jaxpr/tkgd,skd->kgts/dot_general | solution.py:72
  183.5 3.4 %fusion.38 = f32[2,2,256]{2,1,0:T(2,128)S(1)} fusion(f32[2,1024,256,2]{2,1,3,0:T(8,128)} %get-tuple-element.185, f32[2,2,256]{2,1,0:T(2,128)S(1)} %fusion.37, pred[256,1024]{0,1:T(8,128)(4,1)S(1)} %broadcast_compare_fusion.2), kind=kLoop, calls=%fused_computation.4.clone.1 | loop fusion | flops 5241856 | bytes 4464640 | tf_op jit(solution)/shard_map/while/body/eval_jaxpr/reduce_sum | solution.py:80
  186.9 0.0 copy-done
  187.0 2.7 %fusion.40 = f32[2,2,256,128]{3,2,1,0:T(8,128)S(1)} fusion(f32[2,1024,256,2]{2,1,3,0:T(8,128)S(1)} %copy-done, f32[2,2,256]{2,1,0:T(2,128)S(1)} %fusion.37, pred[256,1024]{0,1:T(8,128)(4,1)S(1)} %broadcast_compare_fusion.2, f32[2,2,256,128]{3,2,1,0:T(8,128)S(1)} %get-tuple-element.205, bf16[8192,2,128]{2,0,1:T(8,128)(2,1)} %get-tuple-element.225, ...), kind=kOutput, calls=%fused_computation.7.clone.1 | convolution fusion | flops 274071552 | bytes 6037509 | tf_op jit(solution)/shard_map/while/body/eval_jaxpr/kgts,skd->kgtd/dot_general | solution.py:81
  189.7 0.6 dynamic_slice.33
  190.9 0.2 broadcast_compare_fusion.2
  191.1 3.8 %fusion.36 = (f32[2,2,256]{2,1,0:T(2,128)S(1)}, f32[2,1024,256,2]{2,1,3,0:T(8,128)}) fusion(pred[256,1024]{0,1:T(8,128)(4,1)S(1)} %broadcast_compare_fusion.2, bf16[256,2,2,128]{3,0,2,1:T(8,128)(2,1)S(1)} %get-tuple-element.224, bf16[8192,2,128]{2,0,1:T(8,128)(2,1)} %get-tuple-element.223, s32[]{:T(128)S(6)} %select_n.46), kind=kOutput, calls=%fused_computation.2.clone.1 | convolution fusion | flops 271580160 | bytes 5246980 | tf_op jit(solution)/shard_map/while/body/eval_jaxpr/tkgd,skd->kgts/dot_general | solution.py:72
  194.9 3.4 %fusion.38 = f32[2,2,256]{2,1,0:T(2,128)S(1)} fusion(f32[2,1024,256,2]{2,1,3,0:T(8,128)} %get-tuple-element.185, f32[2,2,256]{2,1,0:T(2,128)S(1)} %fusion.37, pred[256,1024]{0,1:T(8,128)(4,1)S(1)} %broadcast_compare_fusion.2), kind=kLoop, calls=%fused_computation.4.clone.1 | loop fusion | flops 5241856 | bytes 4464640 | tf_op jit(solution)/shard_map/while/body/eval_jaxpr/reduce_sum | solution.py:80
  198.3 0.0 copy-done
  198.4 2.7 %fusion.40 = f32[2,2,256,128]{3,2,1,0:T(8,128)S(1)} fusion(f32[2,1024,256,2]{2,1,3,0:T(8,128)S(1)} %copy-done, f32[2,2,256]{2,1,0:T(2,128)S(1)} %fusion.37, pred[256,1024]{0,1:T(8,128)(4,1)S(1)} %broadcast_compare_fusion.2, f32[2,2,256,128]{3,2,1,0:T(8,128)S(1)} %get-tuple-element.205, bf16[8192,2,128]{2,0,1:T(8,128)(2,1)} %get-tuple-element.225, ...), kind=kOutput, calls=%fused_computation.7.clone.1 | convolution fusion | flops 274071552 | bytes 6037509 | tf_op jit(solution)/shard_map/while/body/eval_jaxpr/kgts,skd->kgtd/dot_general | solution.py:81
  201.1 0.6 dynamic_slice.33
  202.3 0.2 broadcast_compare_fusion.2
  202.6 3.8 %fusion.36 = (f32[2,2,256]{2,1,0:T(2,128)S(1)}, f32[2,1024,256,2]{2,1,3,0:T(8,128)}) fusion(pred[256,1024]{0,1:T(8,128)(4,1)S(1)} %broadcast_compare_fusion.2, bf16[256,2,2,128]{3,0,2,1:T(8,128)(2,1)S(1)} %get-tuple-element.224, bf16[8192,2,128]{2,0,1:T(8,128)(2,1)} %get-tuple-element.223, s32[]{:T(128)S(6)} %select_n.46), kind=kOutput, calls=%fused_computation.2.clone.1 | convolution fusion | flops 271580160 | bytes 5246980 | tf_op jit(solution)/shard_map/while/body/eval_jaxpr/tkgd,skd->kgts/dot_general | solution.py:72
  206.4 3.4 %fusion.38 = f32[2,2,256]{2,1,0:T(2,128)S(1)} fusion(f32[2,1024,256,2]{2,1,3,0:T(8,128)} %get-tuple-element.185, f32[2,2,256]{2,1,0:T(2,128)S(1)} %fusion.37, pred[256,1024]{0,1:T(8,128)(4,1)S(1)} %broadcast_compare_fusion.2), kind=kLoop, calls=%fused_computation.4.clone.1 | loop fusion | flops 5241856 | bytes 4464640 | tf_op jit(solution)/shard_map/while/body/eval_jaxpr/reduce_sum | solution.py:80
  209.7 0.0 copy-done
  209.8 2.7 %fusion.40 = f32[2,2,256,128]{3,2,1,0:T(8,128)S(1)} fusion(f32[2,1024,256,2]{2,1,3,0:T(8,128)S(1)} %copy-done, f32[2,2,256]{2,1,0:T(2,128)S(1)} %fusion.37, pred[256,1024]{0,1:T(8,128)(4,1)S(1)} %broadcast_compare_fusion.2, f32[2,2,256,128]{3,2,1,0:T(8,128)S(1)} %get-tuple-element.205, bf16[8192,2,128]{2,0,1:T(8,128)(2,1)} %get-tuple-element.225, ...), kind=kOutput, calls=%fused_computation.7.clone.1 | convolution fusion | flops 274071552 | bytes 6037509 | tf_op jit(solution)/shard_map/while/body/eval_jaxpr/kgts,skd->kgtd/dot_general | solution.py:81
  212.5 0.2 copy.28
  212.8 3.7 %convolution_convert_fusion = bf16[256,4608]{1,0:T(8,128)(2,1)S(1)} fusion(bf16[256,512]{0,1:T(8,128)(2,1)S(1)} %bitcast.63, bf16[512,4608]{1,0:T(8,128)(2,1)} %param.11), kind=kOutput, calls=%fused_computation.25 | convolution fusion | flops 1209139200 | bytes 7340032 | tf_op jit(solution)/shard_map/dot_general | solution.py:104
  216.5 2.5 copy.29
  219.0 33.0 %all_to_all.5 = bf16[8,256,576]{1,2,0:T(8,128)(2,1)S(1)} all-to-all(bf16[8,256,576]{1,2,0:T(8,128)(2,1)} %bitcast.62), channel_id=1, replica_groups=mesh['ctx_0'=8,'ctx_1'=2,'ctx_2'=2,'head'=8] {'head'}, dimensions={0} | all-to-all | bytes 4718592 | tf_op jit(solution)/shard_map/all_to_all | solution.py:52
  252.0 1.1 reduce_sum.21
  (50 shorter events, 0.4 us)
Async XLA Ops:
  6.5 108.9 %all-gather.5.cloned.1.call-start = ((), (), s32[]{:S(2)}) async-start(), calls=%async_computation.1 | async-start | bytes 8650752 | tf_op jit(solution)/shard_map/all_gather | solution.py:38
  57.3 63.8 %copy-start.1 = (s32[256]{0:T(256)S(1)}, s32[256]{0:T(256)}, u32[]{:S(2)}) copy-start(s32[256]{0:T(256)} %param.10) | copy-start | bytes 3076
  126.4 3.4 %copy-start = (f32[2,1024,256,2]{2,1,3,0:T(8,128)S(1)}, f32[2,1024,256,2]{2,1,3,0:T(8,128)}, u32[]{:S(2)}) copy-start(f32[2,1024,256,2]{2,1,3,0:T(8,128)} %get-tuple-element.185) | copy-start | bytes 12582916 | tf_op jit(solution)/shard_map/while
  137.8 3.4 %copy-start = (f32[2,1024,256,2]{2,1,3,0:T(8,128)S(1)}, f32[2,1024,256,2]{2,1,3,0:T(8,128)}, u32[]{:S(2)}) copy-start(f32[2,1024,256,2]{2,1,3,0:T(8,128)} %get-tuple-element.185) | copy-start | bytes 12582916 | tf_op jit(solution)/shard_map/while
  149.2 3.4 %copy-start = (f32[2,1024,256,2]{2,1,3,0:T(8,128)S(1)}, f32[2,1024,256,2]{2,1,3,0:T(8,128)}, u32[]{:S(2)}) copy-start(f32[2,1024,256,2]{2,1,3,0:T(8,128)} %get-tuple-element.185) | copy-start | bytes 12582916 | tf_op jit(solution)/shard_map/while
  160.7 3.4 %copy-start = (f32[2,1024,256,2]{2,1,3,0:T(8,128)S(1)}, f32[2,1024,256,2]{2,1,3,0:T(8,128)}, u32[]{:S(2)}) copy-start(f32[2,1024,256,2]{2,1,3,0:T(8,128)} %get-tuple-element.185) | copy-start | bytes 12582916 | tf_op jit(solution)/shard_map/while
  172.1 3.4 %copy-start = (f32[2,1024,256,2]{2,1,3,0:T(8,128)S(1)}, f32[2,1024,256,2]{2,1,3,0:T(8,128)}, u32[]{:S(2)}) copy-start(f32[2,1024,256,2]{2,1,3,0:T(8,128)} %get-tuple-element.185) | copy-start | bytes 12582916 | tf_op jit(solution)/shard_map/while
  183.5 3.4 %copy-start = (f32[2,1024,256,2]{2,1,3,0:T(8,128)S(1)}, f32[2,1024,256,2]{2,1,3,0:T(8,128)}, u32[]{:S(2)}) copy-start(f32[2,1024,256,2]{2,1,3,0:T(8,128)} %get-tuple-element.185) | copy-start | bytes 12582916 | tf_op jit(solution)/shard_map/while
  194.9 3.4 %copy-start = (f32[2,1024,256,2]{2,1,3,0:T(8,128)S(1)}, f32[2,1024,256,2]{2,1,3,0:T(8,128)}, u32[]{:S(2)}) copy-start(f32[2,1024,256,2]{2,1,3,0:T(8,128)} %get-tuple-element.185) | copy-start | bytes 12582916 | tf_op jit(solution)/shard_map/while
  206.3 3.4 %copy-start = (f32[2,1024,256,2]{2,1,3,0:T(8,128)S(1)}, f32[2,1024,256,2]{2,1,3,0:T(8,128)}, u32[]{:S(2)}) copy-start(f32[2,1024,256,2]{2,1,3,0:T(8,128)} %get-tuple-element.185) | copy-start | bytes 12582916 | tf_op jit(solution)/shard_map/while
Sparse Core Ops, SparseCore 0:
  10.2 105.2 all-gather.4
where the time goes:
time: 261 us; the launch traced here: 260 us
  blocking collectives  80.1 us (31%)
  waiting for transfers between devices  58.1 us (22%)
  matrix products  55.5 us (21%)
  other arithmetic  30.7 us (12%)
  local copies, waits for them, and re-layouts  16.4 us (6%)
  between operations  13.5 us (5%)
  loops' own time  5.67 us (2%)
    all_gather x1, waiting for transfers between devices, in_one_piece(): lax.all_gather(both, axis, axis=dim, tiled=True)  58.1 us
    all_gather x2, blocking collectives, stacked_from(): pieces = lax.all_gather(pieces, axes[k])  47.1 us
    all_to_all x1, blocking collectives, sent_and_summed(): lax.all_to_all(pieces, axis, split_axis=0, concat_axis=0, tiled=True)  33 us
    dot_general x8, matrix products, attend_block(): jnp.einsum('tkgd,skd->kgts', grouped, key_block, preferred_element_type=j...  30.3 us
    reduce_sum x8, other arithmetic, attend_block(): running_sum = running_sum * decay_old + jnp.sum(weights, axis=-1)  27 us
    dot_general x8, matrix products, attend_block(): jnp.einsum('kgts,skd->kgtd', weights.astype(jnp.bfloat16), value_block, p...  21.4 us
    slice x1, local copies, waits for them, and re-layouts, in_one_piece(): gathered.append(lax.slice_in_dim(out, at, at + a.shape[along], axis=along))  5.7 us
    another operation x1, loops' own time, on_device(): lax.scan(one_block, initial, jnp.arange(piece_rows // block_rows, dtype=j...  5.67 us
  transfers between devices with their start and end apart: 1, of which 1 were waited for; matrix products, arithmetic and copies ran while one was open for 0% of the time, Pallas kernels for 0%

commit v1 on v0

v1 whole, which is shorter than its diff:
```python
import jax
import jax.numpy as jnp
from jax import lax
from jax.experimental import pallas as pl
from jax.experimental.pallas import tpu as pltpu
from jax.sharding import PartitionSpec as P

MESH = pl.DeviceIdType.MESH
NEG_BIG = -1e30
LOG2E = 1.4426950408889634
SCALE = LOG2E / 12.0
NZ = 8
TOK = 256
QUART = 128
HD = 128
STEPS = NZ
STEP_KEYS = 512
ROWS = 512
PAIR = 1152
OUT = 576
XCOLS = 640
F32 = jnp.float32
BF16 = jnp.bfloat16


def kernel(
    q_ref, kv_ref, pos_ref, w_hbm, out_ref,
    kvb, posb, qb, qpos, kb, vtb, pkb, acc, mrun, lrun,
    stage, lstage, attp, lsep, att, w_ref,
    tb, tf, ra, rb, sumf, xs, xr,
    s_kv1, s_kvf, s_pos1, s_posf, s_loc, s_q, s_qp, s_o, s_l, s_a, s_b, s_x,
    r_kv, r_pos, r_q, r_qp, r_o, r_l, r_a, r_b, r_x, w_sem,
):
    ctx, head = lax.axis_index("ctx"), lax.axis_index("head")
    core, xh, z = ctx % 2, (ctx // 2) % 2, ctx // 4
    y, xl = head // 2, head % 2
    other = 1 - core

    def at(zz, xx, cc):
        return ((zz * 2 + xx) * 2 + cc, head)

    z_up, z_down = (z + 1) % NZ, (z + NZ - 1) % NZ
    partner = at(z, xh, other)
    y_up, y_down = (ctx, ((y + 1) % 4) * 2 + xl), (ctx, ((y + 3) % 4) * 2 + xl)
    x_pair = (ctx, y * 2 + 1 - xl)
    peers = [partner, y_up, y_down, x_pair]
    for cc in range(2):
        peers += [at(z_up, xh, cc), at(z_down, xh, cc), at(z, 1 - xh, cc)]
    barrier = pltpu.get_barrier_semaphore()
    for peer in peers:
        pl.semaphore_signal(barrier, inc=1, device_id=peer, device_id_type=MESH)

    w_copy = pltpu.make_async_copy(w_hbm, w_ref, w_sem)
    w_copy.start()

    def remote(src, dst, ssem, rsem, dev):
        return pltpu.make_async_remote_copy(
            src_ref=src, dst_ref=dst, send_sem=ssem, recv_sem=rsem,
            device_id=dev, device_id_type=MESH,
        )

    def kv_own(j, h):
        return kv_ref.at[pl.ds(j * QUART, QUART), pl.ds(h * 256, 256)]

    pl.semaphore_wait(barrier, len(peers))

    own_half = z * 2 + core
    sends = []

    def start(copy):
        copy.start()
        sends.append(copy)

    for j in range(2):
        slot = z * 4 + core * 2 + j
        for h in range(2):
            for d, zz in enumerate((z_up, z_down)):
                if j == 0:
                    start(remote(pos_ref, posb.at[own_half], s_pos1.at[d, h], r_pos.at[own_half], at(zz, xh, h)))
                start(remote(kv_own(j, h), kvb.at[slot], s_kv1.at[d, h, j], r_kv.at[slot], at(zz, xh, h)))
    start(remote(pos_ref, posb.at[own_half], s_pos1.at[2, 0], r_pos.at[own_half], partner))
    for j in range(2):
        slot = z * 4 + core * 2 + j
        lane = pl.multiple_of(other * 256, 256)
        start(remote(kv_ref.at[pl.ds(j * QUART, QUART), pl.ds(lane, 256)], kvb.at[slot], s_loc.at[j], r_kv.at[slot], partner))
    lane = pl.multiple_of(other * 256, 256)
    start(remote(q_ref.at[:, pl.ds(lane, 256)], qb.at[2 + core], s_q.at[2], r_q.at[2 + core], partner))
    start(remote(pos_ref, qpos.at[2 + core], s_qp.at[2], r_qp.at[2 + core], partner))
    for h in range(2):
        dev = at(z, 1 - xh, h)
        start(remote(q_ref.at[:, pl.ds(h * 256, 256)], qb.at[core], s_q.at[h], r_q.at[core], dev))
        start(remote(pos_ref, qpos.at[core], s_qp.at[h], r_qp.at[core], dev))

    lane = pl.multiple_of(core * 256, 256)
    qb[2 + core] = q_ref[:, pl.ds(lane, 256)]
    qpos[2 + core] = pos_ref[...]
    posb[own_half] = pos_ref[...]
    for j in range(2):
        kvb[z * 4 + core * 2 + j] = kv_ref[pl.ds(j * QUART, QUART), pl.ds(lane, 256)]

    mrun[...] = jnp.full(mrun.shape, NEG_BIG, F32)
    lrun[...] = jnp.zeros(lrun.shape, F32)
    acc[...] = jnp.zeros(acc.shape, F32)

    def arrived(step, at_quarter, slot):
        rows = pl.ds(pl.multiple_of(at_quarter * QUART, QUART), QUART)
        kb[step, rows, :] = kvb[slot, :, :HD]
        vtb[step, :, rows] = kvb[slot, :, HD:].T
        lanes = pl.ds(pl.multiple_of((slot % 2) * QUART, QUART), QUART)
        line = posb[slot // 2, :, lanes]
        pkb[step, rows, :] = jnp.broadcast_to(line, (QUART, QUART)).T

    def wait_pos(half):
        remote(posb.at[half], posb.at[half], s_pos1.at[0, 0], r_pos.at[half], partner).wait_recv()

    def wait_kv(slot):
        remote(kvb.at[slot], kvb.at[slot], s_kv1.at[0, 0, 0], r_kv.at[slot], partner).wait_recv()

    for j in range(2):
        arrived(0, core * 2 + j, z * 4 + core * 2 + j)
    wait_pos(z * 2 + other)
    for j in range(2):
        slot = z * 4 + other * 2 + j
        wait_kv(slot)
        arrived(0, other * 2 + j, slot)
    remote(qb.at[2 + other], qb.at[2 + other], s_q.at[0], r_q.at[2 + other], partner).wait_recv()
    remote(qpos.at[2 + other], qpos.at[2 + other], s_qp.at[0], r_qp.at[2 + other], partner).wait_recv()

    def service(i):
        hop, a = i // 4 + 1, i % 4
        step = i // 2 + 1
        for d in range(2):
            src_z = (z + NZ - hop) % NZ if d == 0 else (z + hop) % NZ
            quarter = a if d == 0 else (a + 2) % 4
            slot = src_z * 4 + quarter
            half = slot // 2
            dev = at(z_up if d == 0 else z_down, xh, core)

            @pl.when(a % 2 == 0)
            def _():
                wait_pos(half)

                @pl.when(i < 10)
                def _():
                    remote(posb.at[half], posb.at[half], s_posf.at[d, i // 2], r_pos.at[half], dev).start()

            wait_kv(slot)

            @pl.when(i < 10)
            def _():
                remote(kvb.at[slot], kvb.at[slot], s_kvf.at[d, i], r_kv.at[slot], dev).start()

            arrived(step, (i % 2) * 2 + d, slot)

    def unit(step, g):
        k = kb[step]
        vt = vtb[step]
        pk = pkb[step]
        line = qpos[g]
        mask = jnp.concatenate([pk, pk], axis=1) <= line
        for h in range(2):
            cols = slice(h * TOK, (h + 1) * TOK)
            q = qb[g, :, h * HD:(h + 1) * HD]
            s = lax.dot_general(k, q, (((1,), (1,)), ((), ())), preferred_element_type=F32)
            s = jnp.where(mask, s * SCALE, NEG_BIG)
            m_old = mrun[g, :, cols]
            m_new = jnp.maximum(m_old, jnp.max(s, axis=0, keepdims=True))
            p = jnp.exp2(s - m_new)
            alpha = jnp.exp2(m_old - m_new)
            part = jnp.sum(p.reshape(STEP_KEYS // 8, 8, TOK), axis=0)
            lrun[g, :, cols] = lrun[g, :, cols] * alpha + part
            mrun[g, :, cols] = m_new
            add = jnp.dot(vt, p.astype(BF16), preferred_element_type=F32)
            acc[g, :, cols] = acc[g, :, cols] * alpha + add

    def finalize(g):
        total = jnp.sum(lrun[g], axis=0, keepdims=True)
        lse = mrun[g] + jnp.log2(total)
        o = (acc[g] * (1.0 / total)).astype(BF16)

        @pl.when(g == 2 + core)
        def _():
            attp[0, core] = o
            lsep[0, core] = lse

        @pl.when(g != 2 + core)
        def _():
            stage[g] = o
            lstage[g] = lse

        @pl.when(g < 2)
        def _():
            dev = at(z, 1 - xh, g)
            remote(stage.at[g], attp.at[1, core], s_o.at[g], r_o.at[1, core], dev).start()
            remote(lstage.at[g], lsep.at[1, core], s_l.at[g], r_l.at[1, core], dev).start()

        @pl.when(g == 2 + other)
        def _():
            remote(stage.at[g], attp.at[0, core], s_o.at[2], r_o.at[0, core], partner).start()
            remote(lstage.at[g], lsep.at[0, core], s_l.at[2], r_l.at[0, core], partner).start()

    def body(u, carry):
        early = u < 8
        r = jnp.maximum(u - 8, 0)
        it, w = r // 6, r % 6
        own_g = jnp.where(u % 2 == 0, 2 + other, 2 + core)
        step = jnp.where(early, u // 2, jnp.where(w < 4, 2 * it + w // 2, 4 + it))
        g = jnp.where(early | (w >= 4), own_g, w % 2)

        @pl.when((u >= 1) & early)
        def _():
            service(u - 1)

        @pl.when((u >= 10) & (u <= 28) & ((u - 10) % 3 == 0))
        def _():
            service(7 + (u - 10) // 3)

        @pl.when(u == 8)
        def _():
            for gg in range(2):
                remote(qb.at[gg], qb.at[gg], s_q.at[0], r_q.at[gg], partner).wait_recv()
                remote(qpos.at[gg], qpos.at[gg], s_qp.at[0], r_qp.at[gg], partner).wait_recv()

        unit(step, g)

        @pl.when(u >= 28)
        def _():
            finalize(g)

        return carry

    lax.fori_loop(0, 32, body, 0)

    def wait_part(p, h):
        remote(attp.at[p, h], attp.at[p, h], s_o.at[0], r_o.at[p, h], partner).wait_recv()
        remote(lsep.at[p, h], lsep.at[p, h], s_l.at[0], r_l.at[p, h], partner).wait_recv()

    wait_part(0, other)
    w_copy.wait()
    for h in range(2):
        wait_part(1, h)
        a, b = lsep[0, h], lsep[1, h]
        top = jnp.maximum(a, b)
        wa, wb = jnp.exp2(a - top), jnp.exp2(b - top)
        inv = 1.0 / (wa + wb)
        o = attp[0, h].astype(F32) * (wa * inv) + attp[1, h].astype(F32) * (wb * inv)
        o = o.astype(BF16)
        for hh in range(2):
            lo = (2 * h + hh) * HD
            att[:, lo:lo + HD] = o[:, hh * TOK:(hh + 1) * TOK].T

    def terms(rel, rows):
        cols = pl.ds(pl.multiple_of(((y + rel) % 4) * PAIR, 128), PAIR)
        return jnp.dot(att[rows, :], w_ref[:, cols], preferred_element_type=F32)

    low, high = slice(0, 128), slice(128, 256)
    lo_d, hi_d = pl.ds(0, 128), pl.ds(128, 128)
    tb[1, low, :] = terms(2, low).astype(BF16)
    start(remote(tb.at[1, lo_d], ra.at[0], s_a.at[0], r_a.at[0], y_up))
    tb[1, high, :] = terms(2, high).astype(BF16)
    start(remote(tb.at[1, hi_d], ra.at[1], s_a.at[1], r_a.at[1], y_down))
    tb[0, high, :] = terms(1, high).astype(BF16)
    start(remote(tb.at[0, hi_d], rb.at[0, hi_d], s_b.at[0, 1], r_b.at[0, 1], y_up))
    tb[2, low, :] = terms(3, low).astype(BF16)
    start(remote(tb.at[2, lo_d], rb.at[1, lo_d], s_b.at[1, 0], r_b.at[1, 0], y_down))
    tf[0] = terms(1, low)
    tf[1] = terms(3, high)
    remote(ra.at[0], ra.at[0], s_a.at[0], r_a.at[0], y_down).wait_recv()
    tb[0, low, :] = (tf[0] + ra[0].astype(F32)).astype(BF16)
    start(remote(tb.at[0, lo_d], rb.at[0, lo_d], s_b.at[0, 0], r_b.at[0, 0], y_up))
    remote(ra.at[1], ra.at[1], s_a.at[1], r_a.at[1], y_up).wait_recv()
    tb[2, high, :] = (tf[1] + ra[1].astype(F32)).astype(BF16)
    start(remote(tb.at[2, hi_d], rb.at[1, hi_d], s_b.at[1, 1], r_b.at[1, 1], y_down))
    sumf[...] = terms(0, slice(0, 256))
    give = pl.ds(pl.multiple_of((1 - xl) * 512, 512), XCOLS)
    keep = pl.ds(pl.multiple_of(xl * 512, 512), XCOLS)
    for k, rows in enumerate((slice(0, 128), slice(128, 256))):
        for d in range(2):
            piece = rb.at[d, pl.ds(k * 128, 128)]
            remote(piece, piece, s_b.at[0, 0], r_b.at[d, k], y_down).wait_recv()
        full = sumf[rows, :] + rb[0, rows, :].astype(F32) + rb[1, rows, :].astype(F32)
        sumf[rows, :] = full
        xs[k] = sumf[rows, give].astype(BF16)
        start(remote(xs.at[k], xr.at[k], s_x.at[k], r_x.at[k], x_pair))
    for k, rows in enumerate((slice(0, 128), slice(128, 256))):
        remote(xr.at[k], xr.at[k], s_x.at[k], r_x.at[k], x_pair).wait_recv()
        full = sumf[rows, keep] + xr[k].astype(F32)
        out_ref[rows, :] = jnp.where(xl == 1, full[:, 64:], full[:, :OUT]).astype(BF16)

    for copy in sends:
        copy.wait_send()

    def drain(i, carry):
        for d in range(2):
            remote(kvb.at[0], kvb.at[0], s_kvf.at[d, i], r_kv.at[0], partner).wait_send()

            @pl.when(i % 2 == 0)
            def _():
                remote(posb.at[0], posb.at[0], s_posf.at[d, i // 2], r_pos.at[0], partner).wait_send()
        return carry

    lax.fori_loop(0, 10, drain, 0)
    for k in range(3):
        remote(stage.at[0], stage.at[0], s_o.at[k], r_o.at[0, 0], partner).wait_send()
        remote(lstage.at[0], lstage.at[0], s_l.at[k], r_l.at[0, 0], partner).wait_send()


def on_device(query_heads, key_heads, value_heads, positions, out_weight):
    q = query_heads.reshape(TOK, 4 * HD)
    kv = jnp.stack([key_heads, value_heads], axis=2).reshape(TOK, 4 * HD)
    pos = positions.reshape(1, TOK)
    dma = pltpu.SemaphoreType.DMA
    vmem = pl.BlockSpec(memory_space=pltpu.VMEM)
    return pl.pallas_call(
        kernel,
        out_shape=jax.ShapeDtypeStruct((TOK, OUT), BF16),
        in_specs=[vmem, vmem, vmem, pl.BlockSpec(memory_space=pl.ANY)],
        out_specs=vmem,
        scratch_shapes=[
            pltpu.VMEM((4 * NZ, QUART, 2 * HD), BF16),
            pltpu.VMEM((2 * NZ, 1, TOK), jnp.int32),
            pltpu.VMEM((4, TOK, 2 * HD), BF16),
            pltpu.VMEM((4, 1, TOK), jnp.int32),
            pltpu.VMEM((STEPS, STEP_KEYS, HD), BF16),
            pltpu.VMEM((STEPS, HD, STEP_KEYS), BF16),
            pltpu.VMEM((STEPS, STEP_KEYS, QUART), jnp.int32),
            pltpu.VMEM((4, HD, ROWS), F32),
            pltpu.VMEM((4, 1, ROWS), F32),
            pltpu.VMEM((4, 8, ROWS), F32),
            pltpu.VMEM((4, HD, ROWS), BF16),
            pltpu.VMEM((4, 1, ROWS), F32),
            pltpu.VMEM((2, 2, HD, ROWS), BF16),
            pltpu.VMEM((2, 2, 1, ROWS), F32),
            pltpu.VMEM((TOK, 4 * HD), BF16),
            pltpu.VMEM((4 * HD, 4 * PAIR), BF16),
            pltpu.VMEM((3, TOK, PAIR), BF16),
            pltpu.VMEM((2, 128, PAIR), F32),
            pltpu.VMEM((2, 128, PAIR), BF16),
            pltpu.VMEM((2, TOK, PAIR), BF16),
            pltpu.VMEM((TOK, PAIR), F32),
            pltpu.VMEM((2, 128, XCOLS), BF16),
            pltpu.VMEM((2, 128, XCOLS), BF16),
            dma((2, 2, 2)), dma((2, 10)), dma((3, 2)), dma((2, 5)), dma((2,)),
            dma((3,)), dma((3,)), dma((3,)), dma((3,)), dma((2,)), dma((2, 2)), dma((2,)),
            dma((4 * NZ,)), dma((2 * NZ,)), dma((4,)), dma((4,)), dma((2, 2)), dma((2, 2)),
            dma((2,)), dma((2, 2)), dma((2,)), dma,
        ],
        compiler_params=pltpu.CompilerParams(
            collective_id=0, has_side_effects=True, vmem_limit_bytes=60 * 1024 * 1024
        ),
        cost_estimate=pl.CostEstimate(flops=6_000_000_000, bytes_accessed=6_000_000, transcendentals=8_000_000),
    )(q, kv, pos, out_weight)


def solution(mesh):
    return jax.shard_map(
        on_device,
        mesh=mesh,
        in_specs=(
            P("ctx", "head", None),
            P("ctx", "head", None),
            P("ctx", "head", None),
            P("ctx"),
            P("head", None),
        ),
        out_specs=P("ctx", "head"),
        check_vma=False,
    )
```

time: 261 us -> 93.5 us (0.36)
  Pallas kernels: 0 us -> 87.2 us
  blocking collectives: 80.1 us -> 0 us
  waiting for transfers between devices: 58.1 us -> 0 us
  matrix products: 55.5 us -> 0 us
  other arithmetic: 30.7 us -> 1.36 us
  between operations: 13.5 us -> 0.02 us
  local copies, waits for them, and re-layouts: 16.4 us -> 4.73 us
  loops' own time: 5.67 us -> 0 us
    pallas_call x0 -> x1, Pallas kernels: none -> 87.2 us  [on_device(): pl.pallas_call(kernel, out_shape=jax.ShapeDtypeStruct((TOK, OUT), BF16),...]
    all_gather x1 -> x0, waiting for transfers between devices: 58.1 us -> none  [in_one_piece(): lax.all_gather(both, axis, axis=dim, tiled=True)]
    dot_general x17 -> x0, matrix products: 55.5 us -> none  [the longest x8 30.3 us: attend_block(): jnp.einsum('tkgd,skd->kgts', grouped, key_block, preferred_element_type=j...]
    all_gather x2 -> x0, blocking collectives: 47.1 us -> none  [stacked_from(): pieces = lax.all_gather(pieces, axes[k])]
    all_to_all x1 -> x0, blocking collectives: 33 us -> none  [sent_and_summed(): lax.all_to_all(pieces, axis, split_axis=0, concat_axis=0, tiled=True)]
    reduce_sum x9 -> x0, other arithmetic: 28.1 us -> none  [the longest x8 27 us: attend_block(): running_sum = running_sum * decay_old + jnp.sum(weights, axis=-1)]
    slice x1 -> x0, local copies, waits for them, and re-layouts: 5.7 us -> none  [in_one_piece(): gathered.append(lax.slice_in_dim(out, at, at + a.shape[along], axis=along))]
    another operation x1 -> x0, loops' own time: 5.67 us -> none  [on_device(): lax.scan(one_block, initial, jnp.arange(piece_rows // block_rows, dtype=j...]
  transfers between devices with their start and end apart: 1 -> 0, of which waited for: 1 -> 0; matrix products, arithmetic and copies ran while one was open for 0% -> 0% of each run, Pallas kernels for 0% -> 0%
where the time goes in v1:
time: 93.5 us; the launch traced here: 93.3 us
  Pallas kernels  87.2 us (93%)
  local copies, waits for them, and re-layouts  4.73 us (5%)
  other arithmetic  1.36 us (1%)
    pallas_call x1, Pallas kernels, on_device(): pl.pallas_call(kernel, out_shape=jax.ShapeDtypeStruct((TOK, OUT), BF16),...  87.2 us

profile of v1, /device:TPU:1, one launch (start us, length us, event | category | flops | bytes accessed | tf_op | source)
XLA Modules:
  0.0 93.3 jit_solution(8068958667582927871)
XLA Ops:
  0.0 1.7 %copy.10 = bf16[32,8,4,128]{3,1,2,0:T(8,128)(2,1)} copy(bf16[32,8,4,128]{3,2,1,0:T(4,128)(2,1)} %bitcast.7) | data formatting | bytes 524288
  1.7 1.4 %pad_maximum_fusion = bf16[256,2,2,128]{3,1,0,2:T(2,128)(2,1)S(1)} fusion(bf16[256,2,1,128]{3,1,0,2:T(2,128)(2,1)} %bitcast.9, bf16[256,2,1,128]{3,1,0,2:T(2,128)(2,1)} %bitcast.10), kind=kLoop, calls=%fused_computation.1 | loop fusion | flops 131072 | bytes 524288 | tf_op jit(solution)/shard_map/stack | solution.py:310
  3.1 0.4 copy.6
  3.5 0.8 reshape.10.kv_ref
  4.3 87.2 %shard_map.55 = bf16[256,576]{1,0:T(8,128)(2,1)} custom-call(bf16[256,512]{1,0:T(8,128)(2,1)} %bitcast.8, bf16[256,512]{1,0:T(8,128)(2,1)} %reshape.10.kv_ref, s32[1,256]{1,0:T(1,128)} %bitcast.11, bf16[512,4608]{1,0:T(8,128)(2,1)} %w_hbm.1), custom_call_target="tpu_custom_call" | custom-call | flops 6000000000 | bytes 6000000 | tf_op jit(solution)/shard_map/pallas_call | solution.py:314
  91.5 1.8 %copy.7 = bf16[256,576]{0,1:T(8,128)(2,1)} copy(bf16[256,576]{1,0:T(8,128)(2,1)} %shard_map.55) | data formatting | bytes 589824 | tf_op jit(solution)/shard_map/pallas_call | solution.py:314

commit v2 on v1

v2 whole, which is shorter than its diff:
```python
import jax
import jax.numpy as jnp
from jax import lax
from jax.experimental import pallas as pl
from jax.experimental.pallas import tpu as pltpu
from jax.sharding import PartitionSpec as P

MESH = pl.DeviceIdType.MESH
NEG_BIG = -1e30
LOG2E = 1.4426950408889634
SCALE = LOG2E / 12.0
NZ = 8
TOK = 256
QUART = 128
HD = 128
STEPS = NZ
STEP_KEYS = 512
LANES = 512
OUT = 576
YROWS = 352
XROWS = OUT - YROWS
YCHUNK = YROWS // 2
XHALF = XROWS // 2
F32 = jnp.float32
BF16 = jnp.bfloat16


def kernel(
    q_ref, k_ref, v_ref, pos_ref, w_hbm, out_ref,
    kvs, qs, kvb, posb, qb, qpos, kb, vtb, pkb, acc, mrun, lrun,
    stage, lstage, attp, lsep, att, w_ref, wt,
    tt, ysend, yrecv, xsend, xrecv, dsend, drecv, psend, precv,
    s_kv1, s_kvf, s_pos1, s_posf, s_loc, s_locp, s_q, s_qp, s_o, s_l,
    s_y, s_x, s_d, s_p,
    r_kv, r_pos, r_q, r_qp, r_o, r_l, r_y, r_x, r_d, r_p, w_sem,
):
    ctx, head = lax.axis_index("ctx"), lax.axis_index("head")
    core, xh, z = ctx % 2, (ctx // 2) % 2, ctx // 4
    y, xl = head // 2, head % 2
    other = 1 - core

    def at(zz, xx, cc):
        return ((zz * 2 + xx) * 2 + cc, head)

    z_up, z_down = (z + 1) % NZ, (z + NZ - 1) % NZ
    partner = at(z, xh, other)
    y_next = ((ctx, ((y + 1) % 4) * 2 + xl), (ctx, ((y + 3) % 4) * 2 + xl))
    x_pair = (ctx, y * 2 + 1 - xl)
    peers = [partner, y_next[0], y_next[1], x_pair]
    for cc in range(2):
        peers += [at(z_up, xh, cc), at(z_down, xh, cc), at(z, 1 - xh, cc)]
    barrier = pltpu.get_barrier_semaphore()
    for peer in peers:
        pl.semaphore_signal(barrier, inc=1, device_id=peer, device_id_type=MESH)

    w_copy = pltpu.make_async_copy(w_hbm, w_ref, w_sem)
    w_copy.start()

    for h in range(2):
        kvs[:, h * 256:h * 256 + HD] = k_ref[:, h, :]
        kvs[:, h * 256 + HD:(h + 1) * 256] = v_ref[:, h, :]
        for half in range(2):
            for hh in range(2):
                qs[h, half, hh * 128:(hh + 1) * 128, :] = q_ref[half * 128:(half + 1) * 128, 2 * h + hh, :]

    def remote(src, dst, ssem, rsem, dev):
        return pltpu.make_async_remote_copy(
            src_ref=src, dst_ref=dst, send_sem=ssem, recv_sem=rsem,
            device_id=dev, device_id_type=MESH,
        )

    pl.semaphore_wait(barrier, len(peers))

    sends = []

    def start(copy):
        copy.start()
        sends.append(copy)

    def kv_own(j, h):
        lane = pl.multiple_of(h * 256, 256)
        return kvs.at[pl.ds(j * QUART, QUART), pl.ds(lane, 256)]

    def pos_own(j):
        return pos_ref.at[:, pl.ds(j * QUART, QUART)]

    for n in range(4):
        for d, zz in enumerate((z_up, z_down)):
            j = n // 2 if d == 0 else 1 - n // 2
            h = core if n % 2 == 0 else other
            slot = z * 4 + core * 2 + j
            start(remote(kv_own(j, h), kvb.at[slot], s_kv1.at[d, n], r_kv.at[slot], at(zz, xh, h)))
            start(remote(pos_own(j), posb.at[slot], s_pos1.at[d, n], r_pos.at[slot], at(zz, xh, h)))
    for h in range(2):
        dev = at(z, 1 - xh, h)
        start(remote(qs.at[h], qb.at[core], s_q.at[h], r_q.at[core], dev))
        start(remote(pos_ref, qpos.at[core], s_qp.at[h], r_qp.at[core], dev))
    for j in range(2):
        slot = z * 4 + core * 2 + j
        start(remote(kv_own(j, other), kvb.at[slot], s_loc.at[j], r_kv.at[slot], partner))
        start(remote(pos_own(j), posb.at[slot], s_locp.at[j], r_pos.at[slot], partner))
    start(remote(qs.at[other], qb.at[2 + core], s_q.at[2], r_q.at[2 + core], partner))
    start(remote(pos_ref, qpos.at[2 + core], s_qp.at[2], r_qp.at[2 + core], partner))

    qb[2 + core] = qs[core]
    qpos[2 + core] = pos_ref[...]
    mrun[...] = jnp.full(mrun.shape, NEG_BIG, F32)
    lrun[...] = jnp.zeros(lrun.shape, F32)
    acc[...] = jnp.zeros(acc.shape, F32)

    def place(step, at_quarter, kv, line):
        rows = pl.ds(pl.multiple_of(at_quarter * QUART, QUART), QUART)
        kb[step, rows, :] = kv[:, :HD]
        vtb[step, :, rows] = kv[:, HD:].T
        pkb[step, rows, :] = jnp.broadcast_to(line, (QUART, QUART)).T

    def wait_quarter(slot):
        remote(posb.at[slot], posb.at[slot], s_pos1.at[0, 0], r_pos.at[slot], partner).wait_recv()
        remote(kvb.at[slot], kvb.at[slot], s_kv1.at[0, 0], r_kv.at[slot], partner).wait_recv()

    own_lane = pl.multiple_of(core * 256, 256)
    for j in range(2):
        tokens = slice(j * QUART, (j + 1) * QUART)
        place(0, j, kvs[tokens, pl.ds(own_lane, 256)], pos_ref[:, tokens])
    for j in range(2):
        slot = z * 4 + other * 2 + j
        wait_quarter(slot)
        place(0, 2 + j, kvb[slot], posb[slot])

    w_copy.wait()

    def turn(i, carry):
        cols = pl.ds(pl.multiple_of(i * 128, 128), 128)
        wt[cols, :] = w_ref[:, cols].T
        return carry

    lax.fori_loop(0, 36, turn, 0)

    def service(i, carry):
        hop, a = i // 4 + 1, i % 4
        s = jnp.where(a % 2 == 0, core, other)
        for d in range(2):
            src_z = (z + NZ - hop) % NZ if d == 0 else (z + hop) % NZ
            j = a // 2 if d == 0 else 1 - a // 2
            slot = src_z * 4 + s * 2 + j
            dev = at(z_up if d == 0 else z_down, xh, core)
            wait_quarter(slot)

            @pl.when(i < 10)
            def _():
                remote(kvb.at[slot], kvb.at[slot], s_kvf.at[d, i], r_kv.at[slot], dev).start()
                remote(posb.at[slot], posb.at[slot], s_posf.at[d, i], r_pos.at[slot], dev).start()

            place(i // 2 + 1, (i % 2) * 2 + d, kvb[slot], posb[slot])
        return carry

    def attend(step):
        k = kb[step]
        vt = vtb[step]
        pk = pkb[step]
        blocks = [(g, half) for g in range(4) for half in range(2)]

        def scores(g, half):
            return lax.dot_general(k, qb[g, half], (((1,), (1,)), ((), ())), preferred_element_type=F32)

        s_next = scores(*blocks[0])
        for n, (g, half) in enumerate(blocks):
            s = s_next
            if n + 1 < len(blocks):
                s_next = scores(*blocks[n + 1])
            mask = pk <= qpos[g, :, half * 128:(half + 1) * 128]
            mask = jnp.concatenate([mask, mask], axis=1)
            s = jnp.where(mask, s * SCALE, NEG_BIG)
            cols = slice(half * 256, (half + 1) * 256)
            m_old = mrun[g, :, cols]
            m_new = jnp.maximum(m_old, jnp.max(s, axis=0, keepdims=True))
            p = jnp.exp2(s - m_new)
            alpha = jnp.exp2(m_old - m_new)
            part = jnp.sum(p.reshape(STEP_KEYS // 8, 8, 256), axis=0)
            lrun[g, :, cols] = lrun[g, :, cols] * alpha + part
            mrun[g, :, cols] = m_new
            add = jnp.dot(vt, p.astype(BF16), preferred_element_type=F32)
            acc[g, :, cols] = acc[g, :, cols] * alpha + add

    def round_of(j, done):
        until = jnp.where(j == 0, 4, jnp.where(j == 1, 5, jnp.where(j == 2, 7, jnp.where(j == 3, 8, jnp.where(j == 4, 9, 2 * j)))))
        lax.fori_loop(done, until, service, 0)

        @pl.when(j == 0)
        def _():
            for g in (2 + other, 0, 1):
                remote(qb.at[g], qb.at[g], s_q.at[0], r_q.at[g], partner).wait_recv()
                remote(qpos.at[g], qpos.at[g], s_qp.at[0], r_qp.at[g], partner).wait_recv()

        attend(j)
        return until

    lax.fori_loop(0, STEPS, round_of, 0)

    def finished(g):
        total = jnp.sum(lrun[g], axis=0, keepdims=True)
        lse = mrun[g] + jnp.log2(total)
        return (acc[g] * (1.0 / total)).astype(BF16), lse

    for g in range(2):
        o, lse = finished(g)
        stage[g] = o
        lstage[g] = lse
        dev = at(z, 1 - xh, g)
        start(remote(stage.at[g], attp.at[1, core], s_o.at[g], r_o.at[1, core], dev))
        start(remote(lstage.at[g], lsep.at[1, core], s_l.at[g], r_l.at[1, core], dev))
    o, lse = finished(2 + other)
    stage[2] = o
    lstage[2] = lse
    start(remote(stage.at[2], attp.at[0, core], s_o.at[2], r_o.at[0, core], partner))
    start(remote(lstage.at[2], lsep.at[0, core], s_l.at[2], r_l.at[0, core], partner))
    o, lse = finished(2 + core)
    attp[0, core] = o
    lsep[0, core] = lse

    def wait_part(p, h):
        remote(attp.at[p, h], attp.at[p, h], s_o.at[0], r_o.at[p, h], partner).wait_recv()
        remote(lsep.at[p, h], lsep.at[p, h], s_l.at[0], r_l.at[p, h], partner).wait_recv()

    wait_part(0, other)
    for h in range(2):
        wait_part(1, h)
        a, b = lsep[0, h], lsep[1, h]
        top = jnp.maximum(a, b)
        wa, wb = jnp.exp2(a - top), jnp.exp2(b - top)
        inv = 1.0 / (wa + wb)
        o = (attp[0, h].astype(F32) * (wa * inv) + attp[1, h].astype(F32) * (wb * inv)).astype(BF16)
        for half in range(2):
            for hh in range(2):
                lo = (2 * h + hh) * HD
                frm = half * 256 + hh * 128
                att[lo:lo + HD, half * 128:(half + 1) * 128] = o[:, frm:frm + 128]

    def terms(rel, b):
        row = ((y + rel) % 4) * (2 * OUT) + (xl if b == 0 else 1 - xl) * OUT
        rows = pl.ds(pl.multiple_of(row, 64), OUT)
        t = jnp.dot(wt[rows, :], att[...], preferred_element_type=F32)
        tt[rel * 2 + b] = t

    def chunk(k):
        return slice(k * YCHUNK, (k + 1) * YCHUNK), pl.ds(k * YCHUNK, YCHUNK)

    def send_y(kind, d, k):
        rows = chunk(k)[1]
        start(remote(ysend.at[kind, d, rows], yrecv.at[kind, d, rows], s_y.at[kind, d, k], r_y.at[kind, d, k], y_next[d]))

    def wait_y(kind, d, k):
        piece = yrecv.at[kind, d, chunk(k)[1]]
        remote(piece, piece, s_y.at[0, 0, 0], r_y.at[kind, d, k], x_pair).wait_recv()
        return yrecv[kind, d, chunk(k)[0], :].astype(F32)

    def send_x(rel):
        xsend[rel] = tt[rel * 2 + 1, YROWS:, :].astype(BF16)
        start(remote(xsend.at[rel], xrecv.at[rel], s_x.at[rel], r_x.at[rel], x_pair))

    def wait_x(rel):
        remote(xrecv.at[rel], xrecv.at[rel], s_x.at[0], r_x.at[rel], x_pair).wait_recv()
        tt[rel * 2, YROWS:, :] = tt[rel * 2, YROWS:, :] + xrecv[rel].astype(F32)

    def send_d(kind, d):
        start(remote(dsend.at[kind, d], drecv.at[kind, d], s_d.at[kind, d], r_d.at[kind, d], y_next[d]))

    def wait_d(kind, d):
        remote(drecv.at[kind, d], drecv.at[kind, d], s_d.at[0, 0], r_d.at[kind, d], x_pair).wait_recv()
        return drecv[kind, d].astype(F32)

    halves = (slice(YROWS, YROWS + XHALF), slice(YROWS + XHALF, OUT))

    terms(2, 1)
    ysend[0, 1] = tt[5, :YROWS, :].astype(BF16)
    send_y(0, 1, 0)
    send_y(0, 1, 1)
    send_x(2)
    terms(2, 0)
    ysend[0, 0] = tt[4, :YROWS, :].astype(BF16)
    send_y(0, 0, 0)
    send_y(0, 0, 1)
    terms(1, 1)
    ysend[1, 0] = tt[3, :YROWS, :].astype(BF16)
    send_y(1, 0, 0)
    send_y(1, 0, 1)
    send_x(1)
    terms(3, 0)
    ysend[1, 1] = tt[6, :YROWS, :].astype(BF16)
    send_y(1, 1, 0)
    send_y(1, 1, 1)
    terms(3, 1)
    send_x(3)
    terms(1, 0)
    terms(0, 1)
    send_x(0)
    terms(0, 0)
    wait_x(2)
    for d in range(2):
        dsend[0, d] = tt[4, halves[d], :].astype(BF16)
        send_d(0, d)
    for k in range(2):
        rows = chunk(k)[0]
        for d, n in ((0, 2), (1, 7)):
            got = wait_y(0, d, k)
            ysend[2, d, rows, :] = (tt[n, rows, :] + got).astype(BF16)
            send_y(2, d, k)
    for d, rel in ((0, 1), (1, 3)):
        wait_x(rel)
        dsend[1, d] = tt[2 * rel, halves[1 - d], :].astype(BF16)
        send_d(1, d)
    for d, rel in ((0, 1), (1, 3)):
        got = wait_d(0, d)
        dsend[2, d] = (tt[2 * rel, halves[d], :] + got).astype(BF16)
        send_d(2, d)
    wait_x(0)
    for k in range(2):
        rows = chunk(k)[0]
        full = tt[1, rows, :] + wait_y(1, 0, k) + wait_y(2, 1, k)
        psend[rows, :] = full.astype(BF16)
        start(remote(psend.at[chunk(k)[1]], precv.at[chunk(k)[1]], s_p.at[k], r_p.at[k], x_pair))
        tt[0, rows, :] = tt[0, rows, :] + wait_y(2, 0, k) + wait_y(1, 1, k)
    for d in range(2):
        full = tt[0, halves[d], :] + wait_d(2, d) + wait_d(1, 1 - d)
        out_ref[halves[d], :] = full.astype(BF16)
    for k in range(2):
        rows = chunk(k)[0]
        piece = precv.at[chunk(k)[1]]
        remote(piece, piece, s_p.at[0], r_p.at[k], x_pair).wait_recv()
        out_ref[rows, :] = (tt[0, rows, :] + precv[rows, :].astype(F32)).astype(BF16)

    for copy in sends:
        copy.wait_send()

    def drain(i, carry):
        for d in range(2):
            remote(kvb.at[0], kvb.at[0], s_kvf.at[d, i], r_kv.at[0], partner).wait_send()
            remote(posb.at[0], posb.at[0], s_posf.at[d, i], r_pos.at[0], partner).wait_send()
        return carry

    lax.fori_loop(0, 10, drain, 0)


def on_device(query_heads, key_heads, value_heads, positions, out_weight):
    pos = positions.reshape(1, TOK)
    dma = pltpu.SemaphoreType.DMA
    vmem = pl.BlockSpec(memory_space=pltpu.VMEM)
    out = pl.pallas_call(
        kernel,
        out_shape=jax.ShapeDtypeStruct((OUT, TOK), BF16),
        in_specs=[vmem, vmem, vmem, vmem, pl.BlockSpec(memory_space=pl.ANY)],
        out_specs=vmem,
        scratch_shapes=[
            pltpu.VMEM((TOK, 4 * HD), BF16),
            pltpu.VMEM((2, 2, 256, HD), BF16),
            pltpu.VMEM((4 * NZ, QUART, 2 * HD), BF16),
            pltpu.VMEM((4 * NZ, 1, QUART), jnp.int32),
            pltpu.VMEM((4, 2, 256, HD), BF16),
            pltpu.VMEM((4, 1, TOK), jnp.int32),
            pltpu.VMEM((STEPS, STEP_KEYS, HD), BF16),
            pltpu.VMEM((STEPS, HD, STEP_KEYS), BF16),
            pltpu.VMEM((STEPS, STEP_KEYS, QUART), jnp.int32),
            pltpu.VMEM((4, HD, LANES), F32),
            pltpu.VMEM((4, 1, LANES), F32),
            pltpu.VMEM((4, 8, LANES), F32),
            pltpu.VMEM((3, HD, LANES), BF16),
            pltpu.VMEM((3, 1, LANES), F32),
            pltpu.VMEM((2, 2, HD, LANES), BF16),
            pltpu.VMEM((2, 2, 1, LANES), F32),
            pltpu.VMEM((4 * HD, TOK), BF16),
            pltpu.VMEM((4 * HD, 8 * OUT), BF16),
            pltpu.VMEM((8 * OUT, 4 * HD), BF16),
            pltpu.VMEM((8, OUT, TOK), F32),
            pltpu.VMEM((3, 2, YROWS, TOK), BF16),
            pltpu.VMEM((3, 2, YROWS, TOK), BF16),
            pltpu.VMEM((4, XROWS, TOK), BF16),
            pltpu.VMEM((4, XROWS, TOK), BF16),
            pltpu.VMEM((3, 2, XHALF, TOK), BF16),
            pltpu.VMEM((3, 2, XHALF, TOK), BF16),
            pltpu.VMEM((YROWS, TOK), BF16),
            pltpu.VMEM((YROWS, TOK), BF16),
            dma((2, 4)), dma((2, 10)), dma((2, 4)), dma((2, 10)), dma((2,)), dma((2,)),
            dma((3,)), dma((3,)), dma((3,)), dma((3,)),
            dma((3, 2, 2)), dma((4,)), dma((3, 2)), dma((2,)),
            dma((4 * NZ,)), dma((4 * NZ,)), dma((4,)), dma((4,)), dma((2, 2)), dma((2, 2)),
            dma((3, 2, 2)), dma((4,)), dma((3, 2)), dma((2,)), dma,
        ],
        compiler_params=pltpu.CompilerParams(
            collective_id=0, has_side_effects=True, vmem_limit_bytes=60 * 1024 * 1024
        ),
        cost_estimate=pl.CostEstimate(flops=6_000_000_000, bytes_accessed=6_000_000, transcendentals=8_000_000),
    )(query_heads, key_heads, value_heads, pos, out_weight)
    return out.T


def solution(mesh):
    return jax.shard_map(
        on_device,
        mesh=mesh,
        in_specs=(
            P("ctx", "head", None),
            P("ctx", "head", None),
            P("ctx", "head", None),
            P("ctx"),
            P("head", None),
        ),
        out_specs=P("ctx", "head"),
        check_vma=False,
    )
```

time: 93.5 us -> 68.6 us (0.73)
  Pallas kernels: 87.2 us -> 66.8 us
  local copies, waits for them, and re-layouts: 4.73 us -> 1.69 us
  other arithmetic: 1.36 us -> 0 us
    pallas_call x1, Pallas kernels: 87.2 us -> 66.8 us  [on_device(): pl.pallas_call(kernel, out_shape=jax.ShapeDtypeStruct((OUT, TOK), BF16),...]
    pallas_call x1 -> x0, local copies, waits for them, and re-layouts: 1.84 us -> none  [on_device(): pl.pallas_call(kernel, out_shape=jax.ShapeDtypeStruct((TOK, OUT), BF16),...]
    another operation x1 -> x0, other arithmetic: 1.36 us -> none  [on_device(): kv = jnp.stack([key_heads, value_heads], axis=2).reshape(TOK, 4 * HD)]
where the time goes in v2:
time: 68.6 us; the launch traced here: 68.5 us
  Pallas kernels  66.8 us (97%)
  local copies, waits for them, and re-layouts  1.69 us (2%)
    pallas_call x1, Pallas kernels, on_device(): pl.pallas_call(kernel, out_shape=jax.ShapeDtypeStruct((OUT, TOK), BF16),...  66.8 us
    unnamed x1, local copies, waits for them, and re-layouts  1.69 us

profile of v2, /device:TPU:1, one launch (start us, length us, event | category | flops | bytes accessed | tf_op | source)
XLA Modules:
  0.0 68.5 jit_solution(13246274283694968832)
XLA Ops:
  0.0 66.8 %shard_map.55 = bf16[576,256]{1,0:T(8,128)(2,1)} custom-call(bf16[256,4,128]{2,1,0:T(4,128)(2,1)} %q_ref.1, bf16[256,2,128]{2,1,0:T(2,128)(2,1)} %k_ref.1, bf16[256,2,128]{2,1,0:T(2,128)(2,1)} %v_ref.1, s32[1,256]{1,0:T(1,128)} %bitcast.3, bf16[512,4608]{1,0:T(8,128)(2,1)} %w_hbm.1), custom_call_target="tpu_custom_call" | custom-call | flops 6000000000 | bytes 6000000 | tf_op jit(solution)/shard_map/pallas_call | solution.py:348
  66.8 1.7 %copy.7 = bf16[256,576]{0,1:T(8,128)(2,1)} copy(bf16[256,576]{0,1:T(8,128)(2,1)} %bitcast.2) | data formatting | bytes 589824
